TPU v7x, 256 devices: a whole 4x4x8 slice. The times are simulated.
256 devices in a mesh: tp: 256 (over z, y, x, core).
Axes of the slice: x: 4, y: 4, z: 8, core: 2. Of those that a mesh axis runs over, the one named last changes fastest.
Arguments:
- hidden_in: bfloat16 [1, 2048, 2048], P(None, 'tp')
- lengths: int32 [1], replicated
- attn_norm: bfloat16 [2, 2048], replicated
- w_query: bfloat16 [2, 2048, 32, 64], replicated
- w_key: bfloat16 [2, 2048, 8, 64], replicated
- w_value: bfloat16 [2, 2048, 8, 64], replicated
- w_out: bfloat16 [2, 32, 64, 2048], replicated
- mlp_norm: bfloat16 [2, 2048], replicated
- w_gate: bfloat16 [2, 2048, 8192], P(None, None, 'tp')
- w_up: bfloat16 [2, 2048, 8192], P(None, None, 'tp')
- w_down: bfloat16 [2, 8192, 2048], P(None, 'tp')
- final_norm: bfloat16 [2048], replicated
Outputs:
- output: bfloat16 [1, 2048, 2048], P(None, 'tp')
All inputs are finite; a program needn't handle non-finite values.
Results may differ from a plain program's by a relative error of at most 0.019148.
Values are sent between devices in bfloat16 or wider.
A program may use at most 768 MiB of HBM per device.

v0:
```python
import jax
import jax.numpy as jnp
from jax import lax
from jax.sharding import PartitionSpec as P

NORM_EPS = 1e-5
ROPE_BASE = 500000.0


def rms_norm(hidden, gain):
    h_wide = hidden.astype(jnp.float32)
    inv_rms = lax.rsqrt(jnp.mean(h_wide * h_wide, axis=-1, keepdims=True) + NORM_EPS)
    return (h_wide * inv_rms * gain.astype(jnp.float32)).astype(jnp.bfloat16)


def rope_tables(positions, head_dim):
    half_dim = head_dim // 2
    inv_freq = ROPE_BASE ** (-2.0 * jnp.arange(half_dim).astype(jnp.float32) / head_dim)
    angles = positions.astype(jnp.float32)[:, None, None] * inv_freq[None, None, :]
    return jnp.cos(angles), jnp.sin(angles)


def rotate(proj, cos_tab, sin_tab):
    half_dim = proj.shape[-1] // 2
    first = proj[..., :half_dim]
    second = proj[..., half_dim:]
    return jnp.concatenate([first * cos_tab - second * sin_tab, second * cos_tab + first * sin_tab], axis=-1)


def attend(q_rot, k_all, v_all, q_pos, lengths):
    head_dim = q_rot.shape[-1]
    key_pos = jnp.arange(k_all.shape[1])
    allowed = (key_pos[None, None, :] <= q_pos[None, :, None]) & (key_pos[None, None, :] < lengths[:, None, None])
    scores = jnp.einsum('bqkgd,bskd->bkgqs', q_rot, k_all, preferred_element_type=jnp.float32) * (head_dim ** -0.5)
    scores = jnp.where(allowed[:, None, None, :, :], scores, -1e30)
    prob_mat = jax.nn.softmax(scores, axis=-1).astype(jnp.bfloat16)
    context = jnp.einsum('bkgqs,bskd->bqkgd', prob_mat, v_all, preferred_element_type=jnp.float32)
    return context.astype(jnp.bfloat16)


def solution(mesh):
    tp_size = mesh.shape['tp']

    def device_fn(hidden_in, lengths, attn_norm, w_query, w_key, w_value, w_out, mlp_norm, w_gate, w_up, w_down, final_norm):
        batch, seq_dev, d_model = hidden_in.shape
        heads = w_query.shape[2]
        head_dim = w_query.shape[3]
        kv_heads = w_key.shape[2]
        groups = heads // kv_heads
        q_pos = lax.axis_index('tp') * seq_dev + jnp.arange(seq_dev)
        cos_tab, sin_tab = rope_tables(q_pos, head_dim)
        hidden = hidden_in
        for layer in range(w_query.shape[0]):
            normed = rms_norm(hidden, attn_norm[layer])
            q_proj = jnp.einsum('bsd,dhe->bshe', normed, w_query[layer], preferred_element_type=jnp.float32)
            k_proj = jnp.einsum('bsd,dhe->bshe', normed, w_key[layer], preferred_element_type=jnp.float32)
            v_proj = jnp.einsum('bsd,dhe->bshe', normed, w_value[layer], preferred_element_type=jnp.float32).astype(jnp.bfloat16)
            q_rot = rotate(q_proj, cos_tab, sin_tab).astype(jnp.bfloat16).reshape(batch, seq_dev, kv_heads, groups, head_dim)
            k_rot = rotate(k_proj, cos_tab, sin_tab).astype(jnp.bfloat16)
            k_all = lax.all_gather(k_rot, 'tp', axis=1, tiled=True)
            v_all = lax.all_gather(v_proj, 'tp', axis=1, tiled=True)
            context = attend(q_rot, k_all, v_all, q_pos, lengths).reshape(batch, seq_dev, heads, head_dim)
            attn_out = jnp.einsum('bshe,hed->bsd', context, w_out[layer], preferred_element_type=jnp.float32)
            hidden = (hidden.astype(jnp.float32) + attn_out).astype(jnp.bfloat16)
            normed = rms_norm(hidden, mlp_norm[layer])
            full_normed = lax.all_gather(normed, 'tp', axis=1, tiled=True)
            gate_proj = jnp.einsum('bsd,df->bsf', full_normed, w_gate[layer], preferred_element_type=jnp.float32)
            up_proj = jnp.einsum('bsd,df->bsf', full_normed, w_up[layer], preferred_element_type=jnp.float32)
            gated_act = (jax.nn.silu(gate_proj) * up_proj).astype(jnp.bfloat16)
            part_out = jnp.einsum('bsf,fd->bsd', gated_act, w_down[layer], preferred_element_type=jnp.float32).astype(jnp.bfloat16)
            part_out = part_out.reshape(batch, tp_size, seq_dev, d_model)
            received = lax.all_to_all(part_out, 'tp', 1, 1, tiled=True)
            mlp_out = jnp.sum(received, axis=1, dtype=jnp.float32)
            hidden = (hidden.astype(jnp.float32) + mlp_out).astype(jnp.bfloat16)
        return rms_norm(hidden, final_norm)

    seq_part = P(None, 'tp', None)
    in_specs = (seq_part, P(), P(), P(), P(), P(), P(), P(), P(None, None, 'tp'), P(None, None, 'tp'), P(None, 'tp', None), P())
    return jax.shard_map(device_fn, mesh=mesh, in_specs=in_specs, out_specs=seq_part, check_vma=False)
```

profile of v0, /device:TPU:1, one launch (start us, length us, event | category | flops | bytes accessed | tf_op | source)
XLA Modules:
  0.0 1151.8 jit_solution(1371151510725842853)
XLA Ops:
  11.8 3.2 fusion.114
  15.7 6.7 fusion.96
  22.7 102.0 %all-gather.9.cloned.1.call-done = bf16[1,2048,8,64]{3,1,2,0:T(8,128)(2,1)} async-done(((bf16[1,8,8,64]{3,1,2,0:T(8,128)(2,1)}), bf16[1,2048,8,64]{3,1,2,0:T(8,128)(2,1)}) %all-gather.9.cloned.1.call-update) | async-done | bytes 2097168 | tf_op jit(solution)/shard_map/all_gather | solution.py:60
  124.7 3.8 fusion.189
  129.0 107.6 %all-gather.17.cloned.1.call-done = bf16[2048,8,64]{2,0,1:T(8,128)(2,1)} async-done(((bf16[8,8,64]{2,0,1:T(8,128)(2,1)}), bf16[2048,8,64]{2,0,1:T(8,128)(2,1)}) %all-gather.17.cloned.1.call-update) | async-done | bytes 2097168 | tf_op jit(solution)/shard_map/all_gather | solution.py:61
  236.6 3.0 fusion.102
  239.6 4.8 multiply_reduce_fusion.1
  245.4 117.1 %all-gather.11.cloned.1.call-done = bf16[1,2048,2048]{2,1,0:T(8,128)(2,1)} async-done(((bf16[1,8,2048]{2,1,0:T(8,128)(2,1)}), bf16[1,2048,2048]{2,1,0:T(8,128)(2,1)}) %all-gather.11.cloned.1.call-update) | async-done | bytes 8388624 | tf_op jit(solution)/shard_map/all_gather | solution.py:66
  362.5 6.0 fusion.10
  368.5 12.8 %convert_bitcast_fusion.1 = bf16[1,256,8,2048]{3,2,0,1:T(8,128)(2,1)} fusion(bf16[1,2048,2048]{2,1,0:T(8,128)(2,1)} %all-gather.11.cloned.1.call-done, f32[2048,32]{0,1:T(8,128)S(1)} %fusion.10, bf16[2,32,2048]{2,1,0:T(8,128)(2,1)S(1)} %copy-done.3, bf16[2,2048,32]{1,2,0:T(8,128)(2,1)S(1)} %copy-done.4), kind=kOutput, calls=%fused_computation.21 | convolution fusion | flops 541458432 | bytes 17301504 | tf_op jit(solution)/shard_map/bsf,fd->bsd/dot_general | solution.py:70
  381.3 196.3 %all_to_all.10 = bf16[1,256,8,2048]{3,2,0,1:T(8,128)(2,1)S(1)} all-to-all(bf16[1,256,8,2048]{3,2,0,1:T(8,128)(2,1)} %convert_bitcast_fusion.1), channel_id=1, replica_groups=mesh['tp'=256] {'tp'}, dimensions={1} | all-to-all | bytes 16777216 | tf_op jit(solution)/shard_map/all_to_all | solution.py:72
  581.6 3.1 fusion.117
  585.1 6.7 fusion.99
  591.9 96.8 %all-gather.13.cloned.1.call-done = bf16[1,2048,8,64]{3,1,2,0:T(8,128)(2,1)} async-done(((bf16[1,8,8,64]{3,1,2,0:T(8,128)(2,1)}), bf16[1,2048,8,64]{3,1,2,0:T(8,128)(2,1)}) %all-gather.13.cloned.1.call-update) | async-done | bytes 2097168 | tf_op jit(solution)/shard_map/all_gather | solution.py:60
  688.7 3.8 fusion.190
  692.9 107.5 %all-gather.19.cloned.1.call-done = bf16[2048,8,64]{2,0,1:T(8,128)(2,1)} async-done(((bf16[8,8,64]{2,0,1:T(8,128)(2,1)}), bf16[2048,8,64]{2,0,1:T(8,128)(2,1)}) %all-gather.19.cloned.1.call-update) | async-done | bytes 2097168 | tf_op jit(solution)/shard_map/all_gather | solution.py:61
  800.4 3.0 fusion.105
  803.4 4.7 multiply_reduce_fusion
  808.9 117.4 %all-gather.15.cloned.1.call-done = bf16[1,2048,2048]{2,1,0:T(8,128)(2,1)} async-done(((bf16[1,8,2048]{2,1,0:T(8,128)(2,1)}), bf16[1,2048,2048]{2,1,0:T(8,128)(2,1)}) %all-gather.15.cloned.1.call-update) | async-done | bytes 8388624 | tf_op jit(solution)/shard_map/all_gather | solution.py:66
  926.3 6.0 fusion.2
  932.2 12.9 %convert_bitcast_fusion = bf16[1,256,8,2048]{3,2,0,1:T(8,128)(2,1)} fusion(bf16[1,2048,2048]{2,1,0:T(8,128)(2,1)} %all-gather.15.cloned.1.call-done, f32[2048,32]{0,1:T(8,128)S(1)} %fusion.2, bf16[2,32,2048]{2,1,0:T(8,128)(2,1)S(1)} %copy-done.3, bf16[2,2048,32]{1,2,0:T(8,128)(2,1)S(1)} %copy-done.4), kind=kOutput, calls=%fused_computation.18 | convolution fusion | flops 541458432 | bytes 17301504 | tf_op jit(solution)/shard_map/bsf,fd->bsd/dot_general | solution.py:70
  945.2 9.5 all-to-all-start.1
  954.7 184.7 %all-to-all-done.1 = bf16[1,256,8,2048]{3,2,0,1:T(8,128)(2,1)} async-done(((bf16[1,256,8,2048]{3,2,0,1:T(8,128)(2,1)}), bf16[1,256,8,2048]{3,2,0,1:T(8,128)(2,1)}, u32[]{:S(2)}, u32[]{:S(2)}) %all-to-all-start.1) | async-done | bytes 8388640 | tf_op jit(solution)/shard_map/all_to_all | solution.py:72
  1139.4 4.7 convert_reduce_fusion
  (57 shorter events, 13.3 us)
Async XLA Ops:
  6.5 9.1 copy-start.1
  6.5 118.2 %all-gather.9.cloned.1.call-start = ((), (), s32[]{:S(2)}) async-start(), calls=%async_computation.2 | async-start | bytes 4210688 | tf_op jit(solution)/shard_map/all_gather | solution.py:60
  11.7 224.9 %all-gather.17.cloned.1.call-start = ((), (), s32[]{:S(2)}) async-start(), calls=%async_computation.6 | async-start | bytes 4210688 | tf_op jit(solution)/shard_map/all_gather | solution.py:61
  15.0 347.6 %all-gather.11.cloned.1.call-start = ((), (), s32[]{:S(2)}) async-start(), calls=%async_computation.3 | async-start | bytes 8421376 | tf_op jit(solution)/shard_map/all_gather | solution.py:66
  15.7 7.0 copy-start.5
  239.6 122.9 %copy-start.2 = (bf16[2,2048,32]{1,2,0:T(8,128)(2,1)S(1)}, bf16[2,2048,32]{1,2,0:T(8,128)(2,1)}, u32[]{:S(2)}) copy-start(bf16[2,2048,32]{1,2,0:T(8,128)(2,1)} %param.20) | copy-start | bytes 786436
  245.1 123.4 %copy-start.3 = (bf16[2,32,2048]{2,1,0:T(8,128)(2,1)S(1)}, bf16[2,32,2048]{2,1,0:T(8,128)(2,1)}, u32[]{:S(2)}) copy-start(bf16[2,32,2048]{2,1,0:T(8,128)(2,1)} %param.22) | copy-start | bytes 786436
  245.1 123.4 %copy-start.4 = (bf16[2,2048,32]{1,2,0:T(8,128)(2,1)S(1)}, bf16[2,2048,32]{1,2,0:T(8,128)(2,1)}, u32[]{:S(2)}) copy-start(bf16[2,2048,32]{1,2,0:T(8,128)(2,1)} %param.21) | copy-start | bytes 786436
  245.1 443.6 %all-gather.13.cloned.1.call-start = ((), (), s32[]{:S(2)}) async-start(), calls=%async_computation.4 | async-start | bytes 4210688 | tf_op jit(solution)/shard_map/all_gather | solution.py:60
  577.7 2.2 copy-start
  581.6 218.8 %all-gather.19.cloned.1.call-start = ((), (), s32[]{:S(2)}) async-start(), calls=%async_computation.7 | async-start | bytes 4210688 | tf_op jit(solution)/shard_map/all_gather | solution.py:61
  584.8 341.5 %all-gather.15.cloned.1.call-start = ((), (), s32[]{:S(2)}) async-start(), calls=%async_computation.5 | async-start | bytes 8421376 | tf_op jit(solution)/shard_map/all_gather | solution.py:66
  945.2 9.5 copy-start.6
  945.2 194.2 %all-to-all-start.1 = ((bf16[1,256,8,2048]{3,2,0,1:T(8,128)(2,1)}), bf16[1,256,8,2048]{3,2,0,1:T(8,128)(2,1)}, u32[]{:S(2)}, u32[]{:S(2)}) async-start(bf16[1,256,8,2048]{3,2,0,1:T(8,128)(2,1)} %convert_bitcast_fusion), calls=%async_computation.1 | async-start | bytes 16777216 | tf_op jit(solution)/shard_map/all_to_all | solution.py:72
Sparse Core Ops, SparseCore 0:
  11.8 112.8 all-gather.8
  128.5 108.0 all-gather.16
  245.2 117.2 all-gather.10
  581.7 106.9 all-gather.12
  692.3 108.0 all-gather.18
  809.0 117.2 all-gather.14
where the time goes:
time: 1160 us; the launch traced here: 1150 us
  waiting for transfers between devices  833 us (72%)
  blocking collectives  196 us (17%)
  matrix products  84.1 us (7%)
  between operations  14.3 us (1%)
  other arithmetic  13.2 us (1%)
    all_gather x2, waiting for transfers between devices, device_fn(): full_normed = lax.all_gather(normed, 'tp', axis=1, tiled=True)  235 us
    all_gather x2, waiting for transfers between devices, device_fn(): v_all = lax.all_gather(v_proj, 'tp', axis=1, tiled=True)  215 us
    all_gather x2, waiting for transfers between devices, device_fn(): k_all = lax.all_gather(k_rot, 'tp', axis=1, tiled=True)  199 us
    all_to_all x1, blocking collectives, device_fn(): received = lax.all_to_all(part_out, 'tp', 1, 1, tiled=True)  196 us
    all_to_all x1, waiting for transfers between devices, device_fn(): received = lax.all_to_all(part_out, 'tp', 1, 1, tiled=True)  185 us
    dot_general x2, matrix products, device_fn(): jnp.einsum('bsf,fd->bsd', gated_act, w_down[layer], preferred_element_typ...  25.8 us
  transfers between devices with their start and end apart: 7, of which 7 were waited for; matrix products, arithmetic and copies ran while one was open for 2% of the time, Pallas kernels for 0%

commit v1 on v0

v1 whole, which is shorter than its diff:
```python
import functools

import jax
import jax.numpy as jnp
from jax import lax
from jax.experimental import pallas as pl
from jax.experimental.pallas import tpu as pltpu
from jax.sharding import PartitionSpec as P

NORM_EPS = 1e-5
ROPE_BASE = 500000.0
NX = 4
PLANE = NX * NX
LANES = 128
CHUNK = 256
NT = (((1,), (1,)), ((), ()))
F32, BF16 = jnp.float32, jnp.bfloat16


def remote(src, dst, send_sem, recv_sem, device):
    return pltpu.make_async_remote_copy(
        src_ref=src, dst_ref=dst, send_sem=send_sem, recv_sem=recv_sem,
        device_id=(device,), device_id_type=pl.DeviceIdType.MESH)


def kernel(nz, h_ref, len_ref, cos_ref, sin_ref, gain_ref, wq_ref, wk_ref, wv_ref, wo_ref, wg_ref, wu_ref, wd_ref,
           out_ref, w_all, wo_v, wqkv, h_all, c_mat, kv_all, rs, ps, hres, zb, qbuf, bd,
           local_sem, w_recv, w_send, d_recv, d_send, h_recv, h_send, kv_recv, kv_send, kvd_recv, kvd_send,
           c_recv, c_send, rs_recv, rs_send):
    layers = wo_ref.shape[0]
    seq_dev, d_model = h_ref.shape
    units = wg_ref.shape[1]
    pack = 3 * units
    half = pack // 2
    rows = nz * seq_dev
    hq = wq_ref.shape[1] // nz
    hd = wk_ref.shape[1] // nz
    nch = d_model // CHUNK
    me = lax.axis_index('tp')
    core = me % 2
    px = (me // 2) % NX
    py = (me // (2 * NX)) % NX
    mp = (me // 2) % PLANE
    mz = me // (2 * PLANE)
    base = mz * (2 * PLANE)
    partner = base + mp * 2 + (1 - core)

    def z_peer(i):
        return ((mz + i) % nz) * (2 * PLANE) + mp * 2 + core

    def pack_copies(l):
        mine = w_all.at[l, core, mp]
        return [pltpu.make_async_copy(ref.at[l], mine.at[pl.ds(i * units, units)], local_sem.at[l, i])
                for i, ref in enumerate((wg_ref, wu_ref, wd_ref))]

    def qkv_copies(l):
        return [
            pltpu.make_async_copy(wq_ref.at[l, pl.ds(mz * hq, hq)], wqkv.at[l, pl.ds(0, hq)], local_sem.at[l, 3]),
            pltpu.make_async_copy(wk_ref.at[l, pl.ds(mz * hd, hd)], wqkv.at[l, pl.ds(hq, hd)], local_sem.at[l, 4]),
            pltpu.make_async_copy(wv_ref.at[l, pl.ds(mz * hd, hd)], wqkv.at[l, pl.ds(hq + hd, hd)], local_sem.at[l, 5]),
        ]

    def wo_copy(l):
        return pltpu.make_async_copy(wo_ref.at[l], wo_v.at[l], local_sem.at[l, 6])

    for l in range(layers):
        for c in pack_copies(l) + qkv_copies(l):
            c.start()
        wo_copy(l).start()

    barrier = pltpu.get_barrier_semaphore()

    def signal(device):
        pl.semaphore_signal(barrier, inc=1, device_id=(device,), device_id_type=pl.DeviceIdType.MESH)

    signal(partner)
    for i in range(1, nz):
        signal(z_peer(i))

    @pl.loop(1, PLANE)
    def _(i):
        signal(base + ((mp + i) % PLANE) * 2 + core)

    pl.semaphore_wait(barrier, 1 + (nz - 1) + (PLANE - 1))

    def slot(h, a1, a2):
        return a2 % NX * NX + a1 % NX if h == 0 else a1 % NX * NX + a2 % NX

    def where_am_i(h):
        return (px, py) if h == 0 else (py, px)

    def at(h, a1, a2):
        return base + slot(h, a1, a2) * 2 + core

    third = half // 3
    SPAN = ((0, half), (half, half))
    FROM_MINUS = ((0, 2 * third), (half, third))
    FROM_PLUS = ((2 * third, third), (half + third, 2 * third))

    def piece(l, c, p, span):
        return w_all.at[l, c, p, pl.ds(*span)]

    def w_copy(l, h, p, span, idx, device):
        ref = piece(l, core, p, span)
        return remote(ref, ref, w_send.at[l], w_recv.at[l, h, idx], device)

    def to_partner(l, p, span):
        ref = piece(l, core, p, span)
        remote(ref, ref, d_send.at[l], d_recv.at[l], partner).start()

    def p1(l):
        for c in pack_copies(l):
            c.wait()
        for h in range(2):
            a1, a2 = where_am_i(h)
            w_copy(l, h, mp, SPAN[h], 0, at(h, a1 + 1, a2)).start()
            w_copy(l, h, mp, SPAN[h], 1, at(h, a1 + NX - 1, a2)).start()
        to_partner(l, mp, (0, pack))

    def p2(l):
        for h in range(2):
            a1, a2 = where_am_i(h)
            low, high = slot(h, a1 + NX - 1, a2), slot(h, a1 + 1, a2)
            w_copy(l, h, low, SPAN[h], 0, me).wait_recv()
            w_copy(l, h, low, FROM_MINUS[h], 2, at(h, a1 + 1, a2)).start()
            w_copy(l, h, high, SPAN[h], 1, me).wait_recv()
            w_copy(l, h, high, FROM_PLUS[h], 3, at(h, a1 + NX - 1, a2)).start()
            to_partner(l, low, SPAN[h])
            to_partner(l, high, SPAN[h])

    def p3(l):
        for h in range(2):
            a1, a2 = where_am_i(h)
            for k in (0, 1, 3, 2):
                p = slot(h, a1 + k, a2)
                if k == 2:
                    w_copy(l, h, p, FROM_MINUS[h], 2, me).wait_recv()
                    w_copy(l, h, p, FROM_PLUS[h], 3, me).wait_recv()
                    to_partner(l, p, SPAN[h])
                w_copy(l, h, p, SPAN[h], 4 + k, at(h, a1, a2 + 1)).start()
                w_copy(l, h, p, SPAN[h], 8 + k, at(h, a1, a2 + NX - 1)).start()

    def p4(l):
        for k in (0, 1, 3, 2):
            for h in range(2):
                a1, a2 = where_am_i(h)
                low, high = slot(h, a1 + k, a2 + NX - 1), slot(h, a1 + k, a2 + 1)
                w_copy(l, h, low, SPAN[h], 4 + k, me).wait_recv()
                w_copy(l, h, low, FROM_MINUS[h], 12 + k, at(h, a1, a2 + 1)).start()
                w_copy(l, h, high, SPAN[h], 8 + k, me).wait_recv()
                w_copy(l, h, high, FROM_PLUS[h], 16 + k, at(h, a1, a2 + NX - 1)).start()
                to_partner(l, low, SPAN[h])
                to_partner(l, high, SPAN[h])

    def p5(l):
        for k in (0, 1, 3, 2):
            for h in range(2):
                a1, a2 = where_am_i(h)
                p = slot(h, a1 + k, a2 + 2)
                w_copy(l, h, p, FROM_MINUS[h], 12 + k, me).wait_recv()
                w_copy(l, h, p, FROM_PLUS[h], 16 + k, me).wait_recv()
                to_partner(l, p, SPAN[h])

    def w_done(l):
        ref = w_all.at[l, 1 - core]
        remote(ref, ref, d_send.at[l], d_recv.at[l], partner).wait_recv()

    def h_copy(l, device):
        ref = h_all.at[l, mz]
        return remote(h_ref if l == 0 else ref, ref, h_send.at[l], h_recv.at[l], device)

    def h_start(l):
        for i in range(1, nz):
            h_copy(l, z_peer(i)).start()

    def h_wait(l):
        if nz > 1:
            ref = h_all.at[l, pl.ds(0, nz - 1)]
            remote(ref, ref, h_send.at[l], h_recv.at[l], me).wait_recv()
        for i in range(nz):
            hres[pl.ds(i * seq_dev, seq_dev)] = h_all[l, i].astype(F32)

    def norm_to_zb(g):
        gain = gain_ref[pl.ds(g, 1)]
        step = min(16, rows)

        @pl.loop(0, rows // step)
        def _(i):
            r = pl.ds(pl.multiple_of(i * step, step), step)
            x = hres[r]
            inv = lax.rsqrt(jnp.mean(x * x, axis=-1, keepdims=True) + NORM_EPS)
            zb[r] = (x * inv * gain).astype(BF16)

    lane = lax.broadcasted_iota(jnp.int32, (rows, LANES), 1)
    low_half = lane < hd

    def rotate(x):
        first = (lane % hd) < hd // 2
        swapped = jnp.where(first, pltpu.roll(x, LANES - hd // 2, 1), pltpu.roll(x, hd // 2, 1))
        return x * cos_ref[...] + swapped * sin_ref[...]

    def kv_copy(l, device):
        ref = kv_all.at[l, core, mp]
        return remote(ref, ref, kv_send.at[l], kv_recv.at[l], device)

    def qkv(l):
        for c in qkv_copies(l):
            c.wait()
        proj = lax.dot_general(zb[...], wqkv[l], NT, preferred_element_type=F32)
        kv = proj[:, hq:hq + 2 * hd]
        kv_all[l, core, mp] = jnp.where(low_half, rotate(kv), kv).astype(BF16)

        @pl.loop(1, PLANE)
        def _(i):
            kv_copy(l, base + ((mp + i) % PLANE) * 2 + core).start()

        for j in range(hq // LANES):
            q = rotate(proj[:, j * LANES:(j + 1) * LANES])
            qbuf[2 * j] = jnp.where(low_half, q, 0.0).astype(BF16)
            qbuf[2 * j + 1] = jnp.where(low_half, pltpu.roll(q, LANES - hd, 1), 0.0).astype(BF16)

    def kv_wait(l):
        ref = kv_all.at[l, core, pl.ds(0, PLANE - 1)]
        remote(ref, ref, kv_send.at[l], kv_recv.at[l], me).wait_recv()
        ref = kv_all.at[l, core]
        remote(ref, ref, kvd_send.at[l], kvd_recv.at[l], partner).start()
        ref = kv_all.at[l, 1 - core]
        remote(ref, ref, kvd_send.at[l], kvd_recv.at[l], partner).wait_recv()

    def c_columns(j):
        return pl.ds(pl.multiple_of(mz * hq + j * LANES, LANES), LANES)

    def attention(l):
        keys = 2 * PLANE * rows
        j = lax.broadcasted_iota(jnp.int32, (1, keys), 1)
        key_pos = ((j // seq_dev) % nz) * (2 * PLANE * seq_dev) + ((j // rows) % PLANE) * (2 * seq_dev) \
            + (j // (PLANE * rows)) * seq_dev + j % seq_dev
        i = lax.broadcasted_iota(jnp.int32, (rows, 1), 0)
        q_pos = (i // seq_dev) * (2 * PLANE * seq_dev) + (mp * 2 + core) * seq_dev + i % seq_dev
        allowed = key_pos <= jnp.minimum(q_pos, len_ref[0] - 1)
        for pair in range(hq // LANES):
            outs = []
            for head in (2 * pair, 2 * pair + 1):
                kv = kv_all[l].reshape(keys, LANES)
                s = lax.dot_general(qbuf[head], kv, NT, preferred_element_type=F32) * (hd ** -0.5)
                s = jnp.where(allowed, s, -1e30)
                e = jnp.exp(s - jnp.max(s, axis=-1, keepdims=True))
                p = (e * (1.0 / jnp.sum(e, axis=-1, keepdims=True))).astype(BF16)
                outs.append(jnp.dot(p, kv, preferred_element_type=F32))
            c = jnp.where(low_half, pltpu.roll(outs[0], LANES - hd, 1), outs[1]).astype(BF16)
            c_mat[l, :, c_columns(pair)] = c
            ref = c_mat.at[l, :, c_columns(pair)]
            for i in range(1, nz):
                remote(ref, ref, c_send.at[l], c_recv.at[l], z_peer(i)).start()

    def out_proj(l):
        if nz > 1:
            ref = c_mat.at[l, :, pl.ds(0, (nz - 1) * hq)]
            remote(ref, ref, c_send.at[l], c_recv.at[l], me).wait_recv()
        wo_copy(l).wait()

        @pl.loop(0, nch)
        def _(n):
            cols = pl.ds(pl.multiple_of(n * CHUNK, CHUNK), CHUNK)
            acc = jnp.dot(c_mat[l], wo_v[l, :, cols], preferred_element_type=F32)
            hres[:, cols] = (hres[:, cols] + acc).astype(BF16).astype(F32)

    group = CHUNK // units
    n_groups = 2 * PLANE // group

    def slab(l, g, first, cols):
        per = PLANE // group
        return w_all[l, g // per, pl.ds((g % per) * group, group), pl.ds(first, units), cols]

    def mlp_units(l):
        block = lax.broadcasted_iota(jnp.int32, (rows, CHUNK), 1) // units

        @pl.loop(0, n_groups)
        def _(g):
            every = pl.ds(0, d_model)
            gate = lax.dot_general(zb[...], slab(l, g, 0, every).reshape(CHUNK, d_model), NT, preferred_element_type=F32)
            up = lax.dot_general(zb[...], slab(l, g, units, every).reshape(CHUNK, d_model), NT, preferred_element_type=F32)
            act = gate * (1.0 / (1.0 + jnp.exp(-gate))) * up
            for b in range(group):
                bd[g, pl.ds(b * rows, rows)] = jnp.where(block == b, act, 0.0).astype(BF16)

    def rs_copy(l, n, i):
        return remote(ps.at[l, n, (mz + i) % nz], rs.at[l, mz, n], rs_send.at[l], rs_recv.at[l], z_peer(i))

    def mlp_down(l):
        @pl.loop(0, nch)
        def _(n):
            cols = pl.ds(pl.multiple_of(n * CHUNK, CHUNK), CHUNK)
            acc = jnp.zeros((rows, CHUNK), F32)
            for g in range(n_groups):
                y = jnp.dot(bd[g], slab(l, g, 2 * units, cols).reshape(CHUNK, CHUNK), preferred_element_type=F32)
                y = y.astype(BF16).astype(F32)
                for b in range(group):
                    acc = acc + y[b * rows:(b + 1) * rows]
            ps[l, n] = acc.reshape(nz, seq_dev, CHUNK)
            for i in range(1, nz):
                rs_copy(l, n, i).start()

    def rs_finish(l, store):
        if nz > 1:
            ref = rs.at[l, pl.ds(0, nz - 1)]
            remote(ref, ref, rs_send.at[l], rs_recv.at[l], me).wait_recv()
        mine = pl.ds(pl.multiple_of(mz * seq_dev, seq_dev), seq_dev)
        for n in range(nch):
            rs[l, mz, n] = ps[l, n, mz]
        for n in range(nch):
            total = rs[l, 0, n]
            for i in range(1, nz):
                total = total + rs[l, i, n]
            cols = pl.ds(n * CHUNK, CHUNK)
            store(cols, (hres[mine, cols] + total).astype(BF16))

    def store_next(l):
        def store(cols, x):
            h_all[l + 1, mz, :, cols] = x
        return store

    def store_last(cols, x):
        hres[pl.ds(0, seq_dev), cols] = x.astype(F32)

    h_all[0, mz] = h_ref[...]
    h_start(0)
    p1(0)
    for l in range(layers):
        last = l == layers - 1
        h_wait(l)
        if l == 0:
            p2(0)
        norm_to_zb(l)
        qkv(l)
        if l == 0:
            p3(0)
        kv_wait(l)
        attention(l)
        p4(l)
        out_proj(l)
        norm_to_zb(layers + l)
        if not last:
            p1(l + 1)
        p5(l)
        w_done(l)
        mlp_units(l)
        mlp_down(l)
        if not last:
            p2(l + 1)
            p3(l + 1)
            rs_finish(l, store_next(l))
            h_start(l + 1)
    rs_finish_rows(rs_finish, layers - 1, hres, mz, seq_dev, out_ref, gain_ref, 2 * layers)

    for l in range(layers):
        ref = w_all.at[l, 0, pl.ds(0, PLANE - 1)]
        remote(ref, ref, w_send.at[l], w_recv.at[l, 0, 0], me).wait_send()
        ref = w_all.at[l, 0]
        remote(ref, ref, d_send.at[l], d_recv.at[l], me).wait_send()
        ref = kv_all.at[l, 0, pl.ds(0, PLANE - 1)]
        remote(ref, ref, kv_send.at[l], kv_recv.at[l], me).wait_send()
        ref = kv_all.at[l, 0]
        remote(ref, ref, kvd_send.at[l], kvd_recv.at[l], me).wait_send()
        if nz > 1:
            ref = h_all.at[l, pl.ds(0, nz - 1)]
            remote(ref, ref, h_send.at[l], h_recv.at[l], me).wait_send()
            ref = c_mat.at[l, :, pl.ds(0, (nz - 1) * hq)]
            remote(ref, ref, c_send.at[l], c_recv.at[l], me).wait_send()
            ref = rs.at[l, pl.ds(0, nz - 1)]
            remote(ref, ref, rs_send.at[l], rs_recv.at[l], me).wait_send()


def rs_finish_rows(rs_finish, l, hres, mz, seq_dev, out_ref, gain_ref, g):
    pieces = []
    rs_finish(l, lambda cols, x: pieces.append(x.astype(F32)))
    x = jnp.concatenate(pieces, axis=1)
    inv = lax.rsqrt(jnp.mean(x * x, axis=-1, keepdims=True) + NORM_EPS)
    out_ref[...] = (x * inv * gain_ref[pl.ds(g, 1)]).astype(BF16)


def solution(mesh):
    nz = mesh.shape['tp'] // (2 * PLANE)

    def device_fn(hidden_in, lengths, attn_norm, w_query, w_key, w_value, w_out, mlp_norm, w_gate, w_up, w_down, final_norm):
        seq_dev, d_model = hidden_in.shape[1:]
        layers, _, heads, hd = w_query.shape
        kv_heads = w_key.shape[2]
        units = w_gate.shape[2]
        assert kv_heads == nz and 2 * hd == LANES and heads % nz == 0
        hq = heads // nz * hd
        rows = nz * seq_dev
        nch = d_model // CHUNK
        n_groups = 2 * PLANE * units // CHUNK
        i, lane = jnp.arange(rows), jnp.arange(LANES)
        pos = (i // seq_dev) * (2 * PLANE * seq_dev) + (lax.axis_index('tp') % (2 * PLANE)) * seq_dev + i % seq_dev
        inv_freq = ROPE_BASE ** (-2.0 * (lane % (hd // 2)).astype(F32) / hd)
        angles = pos.astype(F32)[:, None] * inv_freq[None, :]
        cos = jnp.cos(angles)
        sin = jnp.where(lane % hd < hd // 2, -1.0, 1.0) * jnp.sin(angles)
        gains = jnp.concatenate([attn_norm, mlp_norm, final_norm[None]], axis=0).astype(F32)
        by_rows = lambda w: jnp.transpose(w, (0, 2, 3, 1)).reshape(layers, -1, d_model)
        units_first = lambda w: jnp.transpose(w, (0, 2, 1))
        any_spec, vmem, smem = (pl.BlockSpec(memory_space=s) for s in (pl.ANY, pltpu.VMEM, pltpu.SMEM))
        dma = pltpu.SemaphoreType.DMA
        out = pl.pallas_call(
            functools.partial(kernel, nz),
            name='decoder',
            out_shape=jax.ShapeDtypeStruct((seq_dev, d_model), BF16),
            in_specs=[vmem, smem, vmem, vmem, vmem] + [any_spec] * 7,
            out_specs=vmem,
            scratch_shapes=[
                pltpu.VMEM((layers, 2, PLANE, 3 * units, d_model), BF16),
                pltpu.VMEM((layers, heads * hd, d_model), BF16),
                pltpu.VMEM((layers, hq + 2 * hd, d_model), BF16),
                pltpu.VMEM((layers, nz, seq_dev, d_model), BF16),
                pltpu.VMEM((layers, rows, heads * hd), BF16),
                pltpu.VMEM((layers, 2, PLANE, rows, LANES), BF16),
                pltpu.VMEM((layers, nz, nch, seq_dev, CHUNK), F32),
                pltpu.VMEM((layers, nch, nz, seq_dev, CHUNK), F32),
                pltpu.VMEM((rows, d_model), F32),
                pltpu.VMEM((rows, d_model), BF16),
                pltpu.VMEM((hq // hd, rows, LANES), BF16),
                pltpu.VMEM((n_groups, CHUNK // units * rows, CHUNK), BF16),
                dma((layers, 7)), dma((layers, 2, 20)), dma((layers,)), dma((layers,)), dma((layers,)),
            ] + [dma((layers,))] * 10,
            compiler_params=pltpu.CompilerParams(
                collective_id=0, has_side_effects=True, vmem_limit_bytes=67_043_328),
        )(hidden_in[0], lengths, cos, sin, gains, by_rows(w_query), by_rows(w_key), by_rows(w_value),
          w_out.reshape(layers, heads * hd, d_model), units_first(w_gate), units_first(w_up), w_down)
        return out[None]

    seq_part = P(None, 'tp', None)
    in_specs = (seq_part, P(), P(), P(), P(), P(), P(), P(), P(None, None, 'tp'), P(None, None, 'tp'), P(None, 'tp', None), P())
    return jax.shard_map(device_fn, mesh=mesh, in_specs=in_specs, out_specs=seq_part, check_vma=False)
```

time: 1160 us -> 135 us (0.12)
  waiting for transfers between devices: 833 us -> 0 us
  blocking collectives: 196 us -> 0 us
  Pallas kernels: 0 us -> 130 us
  matrix products: 84.1 us -> 0 us
  between operations: 14.3 us -> 0.67 us
    all_gather x6 -> x0, waiting for transfers between devices: 648 us -> none  [the longest x2 235 us: device_fn(): full_normed = lax.all_gather(normed, 'tp', axis=1, tiled=True)]
    all_to_all x1 -> x0, blocking collectives: 196 us -> none  [device_fn(): received = lax.all_to_all(part_out, 'tp', 1, 1, tiled=True)]
    all_to_all x1 -> x0, waiting for transfers between devices: 185 us -> none  [device_fn(): received = lax.all_to_all(part_out, 'tp', 1, 1, tiled=True)]
    pallas_call x0 -> x1, Pallas kernels: none -> 130 us  [device_fn(): pl.pallas_call(functools.partial(kernel, nz), name='decoder', out_shape=j...]
    dot_general x16 -> x0, matrix products: 84.1 us -> none  [the longest x2 25.8 us: device_fn(): jnp.einsum('bsf,fd->bsd', gated_act, w_down[layer], preferred_element_typ...]
  transfers between devices with their start and end apart: 7 -> 0, of which waited for: 7 -> 0; matrix products, arithmetic and copies ran while one was open for 2% -> 0% of each run, Pallas kernels for 0% -> 0%
where the time goes in v1:
time: 135 us
  Pallas kernels  130 us (96%)
  other arithmetic  2.2 us (2%)
  local copies, waits for them, and re-layouts  2.07 us (2%)
    pallas_call x1, Pallas kernels, device_fn(): pl.pallas_call(functools.partial(kernel, nz), name='decoder', out_shape=j...  130 us

profile of v1, /device:TPU:1, one launch (start us, length us, event | category | flops | bytes accessed | tf_op | source)
XLA Modules:
  0.0 134.9 jit_solution(13382661700620403032)
XLA Ops:
  0.7 0.7 broadcast_in_dim.19
  1.4 1.4 %maximum_convert_fusion.gain_ref = f32[5,2048]{1,0:T(8,128)} fusion(bf16[1,2048]{1,0:T(2,128)(2,1)S(1)} %broadcast_in_dim.19, bf16[2,2048]{1,0:T(2,128)(2,1)} %param.19, bf16[2,2048]{1,0:T(2,128)(2,1)} %param.14), kind=kLoop, calls=%fused_computation.3 | loop fusion | flops 61440 | bytes 61440 | tf_op jit(solution)/shard_map/convert_element_type | solution.py:401
  2.7 0.8 fusion
  3.6 130.0 %decoder.1 = bf16[8,2048]{1,0:T(8,128)(2,1)} custom-call(bf16[8,2048]{1,0:T(8,128)(2,1)} %bitcast.21, s32[1]{0:T(128)S(6)} %copy.14.len_ref, f32[64,128]{1,0:T(8,128)} %get-tuple-element.6.cos_ref, f32[64,128]{1,0:T(8,128)} %get-tuple-element.5.sin_ref, f32[5,2048]{1,0:T(8,128)} %maximum_convert_fusion.gain_ref, bf16[2,2048,2048]{2,1,0:T(8,128)(2,1)} %bitcast.14, ...), custom_call_target="tpu_custom_call" | custom-call | tf_op jit(solution)/shard_map/decoder/pallas_call | solution.py:406
  133.6 1.4 %copy.15 = bf16[1,8,2048]{2,1,0:T(8,128)(2,1)} copy(bf16[1,8,2048]{2,1,0:T(8,128)(2,1)} %bitcast.20) | data formatting | bytes 65536
  (2 shorter events, 0.0 us)
